TPU v7x, 32 devices: a whole 2x2x4 slice. The times are simulated.
32 devices in a mesh: hist: 4 (over z), rows: 2 (over y), dom: 4 (over x, core).
Axes of the slice: x: 2, y: 2, z: 4, core: 2. Of those that a mesh axis runs over, the one named last changes fastest.
Arguments:
- row_index: int32 [4, 32768], P(None, ('hist', 'rows', 'dom')), may hold values from 0 to 510
- col_index: int32 [4, 32768], P(None, ('hist', 'rows', 'dom')), may hold values from 0 to 510
- bin_index: int32 [4, 32768], P(None, ('hist', 'rows', 'dom')), may hold values from 0 to 255
- charge: bfloat16 [32768], P(('hist', 'rows', 'dom')), may hold values from 0.5 to 2
- momentum: float32 [2, 32768], P(None, ('hist', 'rows', 'dom')), may hold values from -6 to 6
- history: bfloat16 [32, 512, 512], P('hist', 'rows'), may hold values from 0 to 2
- kernel_cols: bfloat16 [32, 512, 512], P('hist', 'dom'), may hold values from -0.25 to 0.25
- kernel_rows: bfloat16 [32, 512, 2, 512], P('hist', 'rows'), may hold values from -0.046875 to 0.046875
Outputs:
- momentum_out: float32 [2, 32768], P(None, ('hist', 'rows', 'dom'))
- history_out: bfloat16 [32, 512, 512], P('hist', 'rows')
All inputs are finite; a program needn't handle non-finite values.
Results may differ from a plain program's by a relative error of at most 0.0024.
Values may be sent and summed in bfloat16 or wider, within the bound.
A program may use at most 64 MiB of HBM per device.

v0:
```python
import functools
import jax
import jax.numpy as jnp
from jax import lax
from jax.experimental import pallas as pl
from jax.experimental.pallas import tpu as pltpu
from jax.sharding import PartitionSpec as P

NG = 512
BINS = 16
STEPS = 4
CORES = 2
PIECES = 8
kick_scale = 0.5

MESH = pl.DeviceIdType.MESH
VM = pl.BlockSpec(memory_space=pltpu.VMEM)
NT = (((1,), (1,)), ((), ()))


def place():
    return lax.axis_index("hist"), lax.axis_index("rows"), lax.axis_index("dom")


def hat(first, extent, where):
    places = lax.broadcasted_iota(jnp.int32, (extent, where.shape[1]), 0) + first
    gap = (places.astype(jnp.float32) - where).astype(jnp.bfloat16)
    return jnp.maximum(jnp.bfloat16(1.0) - jnp.abs(gap), jnp.bfloat16(0.0))


def plane_peer(rows, dom, shift):
    h, r, d = place()
    other = lax.rem(r * dom + d + shift, rows * dom)
    return other, (h, other // dom, lax.rem(other, dom))


def plane_barrier(rows, dom):
    barrier = pltpu.get_barrier_semaphore()
    for shift in range(1, rows * dom):
        pl.semaphore_signal(barrier, inc=1, device_id=plane_peer(rows, dom, shift)[1], device_id_type=MESH)
    pl.semaphore_wait(barrier, rows * dom - 1)


def gather_kernel(rows, dom, row_ref, col_ref, bin_ref, charge_ref, spots, out, charges, total,
                  send, recv, send_c, recv_c):
    _, r, d = place()
    n = rows * dom
    _, band, width = out.shape
    bins = bin_ref[...]
    row_bin = bins // BINS
    spots[0, 0:STEPS] = row_ref[...].astype(jnp.float32) + (row_bin.astype(jnp.float32) + 0.5) / BINS
    spots[0, STEPS:] = col_ref[...].astype(jnp.float32) + ((bins - row_bin * BINS).astype(jnp.float32) + 0.5) / BINS
    charges[0] = charge_ref[...]
    plane_barrier(rows, dom)

    def pair(shift):
        _, device = plane_peer(rows, dom, shift)
        return (
            pltpu.make_async_remote_copy(
                src_ref=spots.at[0], dst_ref=spots.at[shift], send_sem=send.at[shift], recv_sem=recv.at[shift],
                device_id=device, device_id_type=MESH),
            pltpu.make_async_remote_copy(
                src_ref=charge_ref, dst_ref=charges.at[shift], send_sem=send_c.at[shift],
                recv_sem=recv_c.at[shift], device_id=device, device_id_type=MESH))

    for shift in range(1, n):
        for copy in pair(shift):
            copy.start()
    total[...] = jnp.zeros_like(total)

    def add(shift):
        charge = charges[shift].astype(jnp.bfloat16)
        for s in range(STEPS):
            row = hat(r * band, band, spots[shift, s:s + 1, :]) * charge
            col = hat(d * width, width, spots[shift, STEPS + s:STEPS + s + 1, :])
            total[STEPS - 1 - s] += lax.dot_general(row, col, NT, preferred_element_type=jnp.float32)

    add(0)

    def step(shift, carry):
        for copy in pair(shift):
            copy.wait_recv()
        add(shift)
        return carry

    lax.fori_loop(1, n, step, 0)
    out[...] = total[...].astype(out.dtype)
    for shift in range(1, n):
        for copy in pair(shift):
            copy.wait_send()


def deposit(row_index, col_index, bin_index, charge, rows, dom, band, width):
    n = rows * dom
    own = row_index.shape[1]
    tile = (STEPS, band, width)
    return pl.pallas_call(
        functools.partial(gather_kernel, rows, dom),
        out_shape=(jax.ShapeDtypeStruct((n, 2 * STEPS, own), jnp.float32),
                   jax.ShapeDtypeStruct(tile, jnp.bfloat16)),
        in_specs=[VM] * 4, out_specs=(VM, VM),
        scratch_shapes=[pltpu.VMEM((n, 1, own), charge.dtype), pltpu.VMEM(tile, jnp.float32)]
        + [pltpu.SemaphoreType.DMA((n,))] * 4,
        compiler_params=pltpu.CompilerParams(collective_id=1, has_side_effects=True),
    )(row_index, col_index, bin_index, charge)


def field_kernel(hist, rows, dom, part, old_ref, cols_ref, rows_ref, parts, own_out, newest,
                 out, arrived, summed, grids, cols, rows_in, total, load,
                 sem_hs, sem_hr, sem_cs, sem_cr, sem_xs, sem_xr, sem_ps, sem_pr, sem_fs, sem_fr):
    lags, width, _ = cols.shape
    band = part.shape[1]
    piece = NG // rows
    loads = (pltpu.make_async_copy(old_ref, grids.at[pl.ds(STEPS, lags)], load.at[0]),
             pltpu.make_async_copy(cols_ref, cols, load.at[1]),
             pltpu.make_async_copy(rows_ref, rows_in, load.at[2]))
    for copy in loads:
        copy.start()
    h, r, d = place()
    chips = dom // CORES
    up, down = (h + 1, r, d), (h - 1, r, d)
    partner = (h, r, d + 1 - 2 * lax.rem(d, CORES))
    is_first, is_last = h == 0, h == hist - 1
    barrier = pltpu.get_barrier_semaphore()

    @pl.when(jnp.logical_not(is_last))
    def _():
        pl.semaphore_signal(barrier, inc=1, device_id=up, device_id_type=MESH)

    @pl.when(jnp.logical_not(is_first))
    def _():
        pl.semaphore_signal(barrier, inc=1, device_id=down, device_id_type=MESH)

    across = [(h, r, lax.rem(d + CORES * j, dom)) for j in range(1, chips)]
    pl.semaphore_signal(barrier, inc=1, device_id=partner, device_id_type=MESH)
    for device in across:
        pl.semaphore_signal(barrier, inc=1, device_id=device, device_id_type=MESH)
    count = chips + jnp.where(is_first, 0, 1) + jnp.where(is_last, 0, 1)
    pl.semaphore_wait(barrier, count)

    def remote(src, dst, s_sem, r_sem, device):
        return pltpu.make_async_remote_copy(src_ref=src, dst_ref=dst, send_sem=s_sem, recv_sem=r_sem,
                                            device_id=device, device_id_type=MESH)

    def tail_copy(c):
        columns = pl.ds(pl.multiple_of(d * width, width), width)
        return remote(old_ref.at[lags - STEPS + c, :, columns], out.at[d, c], sem_hs.at[c], sem_hr.at[c], up)

    def chain_copy(src, c):
        return remote(src.at[c], arrived.at[c], sem_cs.at[c], sem_cr.at[c], down)

    def cross_copy(c, j):
        return remote(out.at[d, c], out.at[d, c], sem_xs.at[c, j], sem_xr.at[c, j], across[j - 1])

    def partner_copy(c):
        return remote(out.at[d, c], out.at[d, c], sem_ps.at[c], sem_pr.at[c], partner)

    def forward_copy(c, j):
        other = lax.rem(d + CORES * (chips - j), dom)
        return remote(out.at[other, c], out.at[other, c], sem_fs.at[c, j], sem_fr.at[c, j], partner)

    @pl.when(is_last)
    def _():
        for c in range(STEPS):
            chain_copy(part, c).start()

    @pl.when(jnp.logical_not(is_last))
    def _():
        for c in range(STEPS):
            tail_copy(c).start()

    def products(k, first, steps):
        window = grids[pl.ds(k + STEPS - first - steps, steps)].reshape(steps * band, NG)
        mixed = lax.dot_general(cols[k], window, NT, preferred_element_type=jnp.float32).astype(part.dtype)
        stacked = jnp.concatenate(
            [mixed[:, (steps - 1 - s) * band:(steps - s) * band] for s in range(steps)], axis=0)
        span = slice(first * width, (first + steps) * width)
        for comp in range(2):
            total[comp, span] += jnp.dot(stacked, rows_in[k, comp], preferred_element_type=jnp.float32)

    def travel():
        for c in range(STEPS):
            @pl.when(jnp.logical_not(is_last))
            def _():
                chain_copy(part, c).wait_recv()
                both = part[c].astype(jnp.float32) + arrived[c].astype(jnp.float32)

                @pl.when(is_first)
                def _():
                    out[d, c] = both.astype(out.dtype)

                @pl.when(jnp.logical_not(is_first))
                def _():
                    summed[c] = both.astype(out.dtype)
                    chain_copy(summed, c).start()

            @pl.when(jnp.logical_not(is_first))
            def _():
                tail_copy(c).wait_recv()

            for j in range(1, chips):
                cross_copy(c, j).start()
            partner_copy(c).start()
        for c in range(STEPS):
            for j in range(1, chips):
                cross_copy(c, j).wait_recv()
                forward_copy(c, j).start()

    def compute():
        total[...] = jnp.zeros_like(total)
        for copy in loads:
            copy.wait()

        def lag(k, carry):
            products(k, 0, STEPS)
            return carry

        lax.fori_loop(STEPS, lags, lag, 0)
        for k in range(1, STEPS):
            products(k, 0, k)

    def phase(turn, carry):
        now = jnp.logical_xor(turn == 0, is_first)

        @pl.when(now)
        def _():
            travel()

        @pl.when(jnp.logical_not(now))
        def _():
            compute()

        return carry

    lax.fori_loop(0, 2, phase, 0)
    for c in range(STEPS):
        partner_copy(c).wait_recv()
        for j in range(1, chips):
            forward_copy(c, j).wait_recv()
    for e in range(dom):
        grids[0:STEPS, :, e * width:(e + 1) * width] = out[e]
    newest[...] = grids[0:STEPS]
    for k in range(STEPS):
        products(k, k, STEPS - k)
    for q in range(rows):
        block = jnp.concatenate([total[comp, :, q * piece:(q + 1) * piece] for comp in range(2)], axis=1)
        parts[q] = block.astype(parts.dtype)

        @pl.when(r == q)
        def _():
            own_out[...] = block

    for c in range(STEPS):
        partner_copy(c).wait_send()
        for j in range(1, chips):
            forward_copy(c, j).wait_send()
            cross_copy(c, j).wait_send()

    @pl.when(jnp.logical_not(is_first))
    def _():
        for c in range(STEPS):
            chain_copy(part, c).wait_send()

    @pl.when(jnp.logical_not(is_last))
    def _():
        for c in range(STEPS):
            tail_copy(c).wait_send()


def field_parts(part, old, kernel_cols, rows_t, hist, rows, dom):
    lags, width, _ = kernel_cols.shape
    band = old.shape[1]
    chips = dom // CORES
    dma = pltpu.SemaphoreType.DMA
    anywhere = pl.BlockSpec(memory_space=pl.ANY)
    wide = (STEPS * width, 2 * NG // rows)
    return pl.pallas_call(
        functools.partial(field_kernel, hist, rows, dom),
        out_shape=(jax.ShapeDtypeStruct((rows,) + wide, jnp.bfloat16),
                   jax.ShapeDtypeStruct(wide, jnp.float32),
                   jax.ShapeDtypeStruct((STEPS, band, NG), old.dtype)),
        in_specs=[VM, anywhere, anywhere, anywhere], out_specs=(VM, VM, VM),
        scratch_shapes=[pltpu.VMEM((dom,) + part.shape, part.dtype), pltpu.VMEM(part.shape, part.dtype),
                        pltpu.VMEM(part.shape, part.dtype),
                        pltpu.VMEM((lags + STEPS, band, NG), old.dtype),
                        pltpu.VMEM(kernel_cols.shape, kernel_cols.dtype),
                        pltpu.VMEM(rows_t.shape, rows_t.dtype),
                        pltpu.VMEM((2, STEPS * width, NG), jnp.float32), dma((3,))]
        + [dma((STEPS,))] * 4 + [dma((STEPS, chips))] * 2 + [dma((STEPS,))] * 2 + [dma((STEPS, chips))] * 2,
        compiler_params=pltpu.CompilerParams(collective_id=2, has_side_effects=True),
    )(part, old, kernel_cols, rows_t)


def sum_kernel(hist, rows, dom, parts, own, spots, momentum, out, got, mine, from_low, from_high, to_high, to_low,
               kicks, got_kicks, sem_ys, sem_yr, sem_us, sem_ur, sem_ds, sem_dr, sem_ks, sem_kr):
    h, r, d = place()
    n = rows * dom
    tall, wide = own.shape
    width, band = tall // STEPS, wide // 2
    size = tall // PIECES
    kind = parts.dtype
    up, down = (h + 1, r, d), (h - 1, r, d)
    is_first, is_last = h == 0, h == hist - 1
    inner = jnp.logical_and(h > 0, h < hist - 1)
    barrier = pltpu.get_barrier_semaphore()

    @pl.when(jnp.logical_not(is_last))
    def _():
        pl.semaphore_signal(barrier, inc=1, device_id=up, device_id_type=MESH)

    @pl.when(jnp.logical_not(is_first))
    def _():
        pl.semaphore_signal(barrier, inc=1, device_id=down, device_id_type=MESH)

    for shift in range(1, n):
        pl.semaphore_signal(barrier, inc=1, device_id=plane_peer(rows, dom, shift)[1], device_id_type=MESH)
    pl.semaphore_wait(barrier, n - 1 + jnp.where(is_first, 0, 1) + jnp.where(is_last, 0, 1))

    def span(c):
        return pl.ds(pl.multiple_of(c * size, size), size)

    def row_copy(c, j):
        other = lax.rem(r + j, rows)
        return pltpu.make_async_remote_copy(
            src_ref=parts.at[other, span(c)], dst_ref=got.at[j, span(c)], send_sem=sem_ys.at[c, j],
            recv_sem=sem_yr.at[c, j], device_id=(h, other, d), device_id_type=MESH)

    def up_copy(c):
        return pltpu.make_async_remote_copy(
            src_ref=to_high.at[span(c)], dst_ref=from_low.at[span(c)], send_sem=sem_us.at[c],
            recv_sem=sem_ur.at[c], device_id=up, device_id_type=MESH)

    def down_copy(c):
        return pltpu.make_async_remote_copy(
            src_ref=to_low.at[span(c)], dst_ref=from_high.at[span(c)], send_sem=sem_ds.at[c],
            recv_sem=sem_dr.at[c], device_id=down, device_id_type=MESH)

    for c in range(PIECES):
        for j in range(1, rows):
            row_copy(c, j).start()

    kicks[...] = jnp.zeros_like(kicks)

    def kick(s):
        rows_s = pl.ds(pl.multiple_of(s * width, width), width)
        value = mine[rows_s]
        stacked = jnp.concatenate([value[:, :band], value[:, band:]], axis=0)
        coarse = stacked.astype(kind)
        fine = (stacked - coarse.astype(jnp.float32)).astype(kind)
        table = jnp.concatenate([coarse, fine], axis=0)

        def block(k, carry):
            row = hat(r * band, band, spots[k, pl.ds(s, 1), :])
            col = hat(d * width, width, spots[k, pl.ds(STEPS + s, 1), :]).astype(jnp.float32)
            along = jnp.dot(table, row, preferred_element_type=jnp.float32)
            for comp in range(2):
                both = (along[comp * width:(comp + 1) * width]
                        + along[(2 + comp) * width:(3 + comp) * width])
                kicks[k, comp:comp + 1, :] += jnp.sum(both * col, axis=0, keepdims=True)
            return carry

        lax.fori_loop(0, n, block, 0, unroll=8)

    lag = 2 * (hist - 2)
    group = PIECES // STEPS
    late = lag + 3

    def step(t, carry):
        @pl.when(t < PIECES)
        def _():
            value = own[span(t)]
            for j in range(1, rows):
                row_copy(t, j).wait_recv()
                value += got[j, span(t)].astype(jnp.float32)
            mine[span(t)] = value

            @pl.when(is_first)
            def _():
                to_high[span(t)] = value.astype(kind)
                up_copy(t).start()

            @pl.when(is_last)
            def _():
                to_low[span(t)] = value.astype(kind)
                down_copy(t).start()

        low = t - 2 * h

        @pl.when(jnp.logical_and(inner, jnp.logical_and(low >= 0, low < PIECES)))
        def _():
            up_copy(low).wait_recv()
            to_high[span(low)] = (mine[span(low)] + from_low[span(low)].astype(jnp.float32)).astype(kind)
            up_copy(low).start()

        high = t - 2 * (hist - 1 - h)

        @pl.when(jnp.logical_and(inner, jnp.logical_and(high >= 0, high < PIECES)))
        def _():
            down_copy(high).wait_recv()
            to_low[span(high)] = (mine[span(high)] + from_high[span(high)].astype(jnp.float32)).astype(kind)
            down_copy(high).start()

        done = t - late

        @pl.when(done >= 0)
        def _():
            @pl.when(is_first)
            def _():
                down_copy(done).wait_recv()
                mine[span(done)] = mine[span(done)] + from_high[span(done)].astype(jnp.float32)

            @pl.when(is_last)
            def _():
                up_copy(done).wait_recv()
                mine[span(done)] = mine[span(done)] + from_low[span(done)].astype(jnp.float32)

            @pl.when(inner)
            def _():
                mine[span(done)] = (mine[span(done)] + from_low[span(done)].astype(jnp.float32)
                                    + from_high[span(done)].astype(jnp.float32))

            @pl.when(lax.rem(done, group) == group - 1)
            def _():
                kick(done // group)

        return carry

    lax.fori_loop(0, PIECES + late, step, 0)

    def kick_copy(k):
        _, device = plane_peer(rows, dom, n - k)
        return pltpu.make_async_remote_copy(
            src_ref=kicks.at[k], dst_ref=got_kicks.at[k], send_sem=sem_ks.at[k], recv_sem=sem_kr.at[k],
            device_id=device, device_id_type=MESH)

    for k in range(1, n):
        kick_copy(k).start()

    def finish(c, carry):
        @pl.when(jnp.logical_not(is_last))
        def _():
            up_copy(c).wait_send()

        @pl.when(jnp.logical_not(is_first))
        def _():
            down_copy(c).wait_send()

        for j in range(1, rows):
            row_copy(c, j).wait_send()
        return carry

    lax.fori_loop(0, PIECES, finish, 0)
    total = kicks[0]
    for k in range(1, n):
        kick_copy(k).wait()
        total = total + got_kicks[k]
    out[...] = momentum[...] + kick_scale * total


def sum_and_kick(parts, own, spots, momentum, hist, rows, dom):
    tall, wide = own.shape
    n = rows * dom
    dma = pltpu.SemaphoreType.DMA
    flat = pltpu.VMEM((tall, wide), parts.dtype)
    each = pltpu.VMEM((n,) + momentum.shape, momentum.dtype)
    return pl.pallas_call(
        functools.partial(sum_kernel, hist, rows, dom),
        out_shape=jax.ShapeDtypeStruct(momentum.shape, momentum.dtype),
        in_specs=[VM] * 4, out_specs=VM,
        scratch_shapes=[pltpu.VMEM(parts.shape, parts.dtype), pltpu.VMEM((tall, wide), jnp.float32),
                        flat, flat, flat, flat, each, each]
        + [dma((PIECES, rows))] * 2 + [dma((PIECES,))] * 4 + [dma((n,))] * 2,
        compiler_params=pltpu.CompilerParams(collective_id=3, has_side_effects=True),
    )(parts, own, spots, momentum)


def local(hist, rows, dom, row_index, col_index, bin_index, charge, momentum, history, kernel_cols, kernel_rows):
    band = history.shape[1]
    width = kernel_cols.shape[1]
    spots, part = deposit(row_index, col_index, bin_index, charge.astype(jnp.float32)[None], rows, dom, band, width)
    rows_t = jnp.transpose(kernel_rows, (0, 2, 1, 3))
    parts, own, newest = field_parts(part, history, kernel_cols, rows_t, hist, rows, dom)
    cycle_now = jnp.concatenate([newest, history[:-STEPS]], axis=0)
    return sum_and_kick(parts, own, spots, momentum, hist, rows, dom), cycle_now


def solution(mesh):
    spread = ("hist", "rows", "dom")
    in_specs = (P(None, spread), P(None, spread), P(None, spread), P(spread), P(None, spread),
                P("hist", "rows", None), P("hist", "dom", None), P("hist", "rows", None, None))
    out_specs = (P(None, spread), P("hist", "rows", None))
    sizes = mesh.shape
    body = functools.partial(local, sizes["hist"], sizes["rows"], sizes["dom"])
    return jax.shard_map(body, mesh=mesh, in_specs=in_specs, out_specs=out_specs, check_vma=False)
```

profile of v0, /device:TPU:0, one launch (start us, length us, event | category | flops | bytes accessed | tf_op | source)
XLA Modules:
  0.0 86.8 jit_solution(1732792044567915365)
XLA Ops:
  0.6 1.3 %broadcast_in_dim.7 = f32[1024]{0:T(1024)} convert(bf16[1024]{0:T(1024)(128)(2,1)} %param.11) | non-fusion elementwise | flops 1024 | bytes 6144 | tf_op jit(solution)/shard_map/broadcast_in_dim | solution.py:480
  1.9 14.1 %shard_map.95 = (f32[8,8,1024]{2,1,0:T(8,128)}, bf16[4,256,128]{2,1,0:T(8,128)(2,1)}) custom-call(s32[4,1024]{1,0:T(4,128)} %row_ref.1, s32[4,1024]{1,0:T(4,128)} %col_ref.1, s32[4,1024]{1,0:T(4,128)} %bin_ref.1, f32[1,1024]{1,0:T(1,128)} %bitcast.5), custom_call_target="tpu_custom_call" | custom-call | tf_op jit(solution)/shard_map/pallas_call | solution.py:97
  16.1 5.0 %copy.12 = bf16[8,256,2,512]{3,1,2,0:T(8,128)(2,1)} copy(bf16[8,256,2,512]{3,2,1,0:T(2,128)(2,1)} %param.15) | data formatting | bytes 8388608 | tf_op args[7]
  21.0 25.6 %shard_map.96 = (bf16[2,512,512]{2,1,0:T(8,128)(2,1)}, f32[512,512]{1,0:T(8,128)}, bf16[4,256,512]{2,1,0:T(8,128)(2,1)}) custom-call(bf16[4,256,128]{2,1,0:T(8,128)(2,1)} %get-tuple-element.7.part, bf16[8,256,512]{2,1,0:T(8,128)(2,1)} %old_ref.1, bf16[8,128,512]{2,1,0:T(8,128)(2,1)} %cols_ref.1, bf16[8,2,256,512]{3,2,1,0:T(8,128)(2,1)} %bitcast.4), custom_call_target="tpu_custom_call" | custom-call | tf_op jit(solution)/shard_map/pallas_call | solution.py:277
  46.7 0.0 slice-start
  46.7 0.0 copy-start
  46.7 38.0 %shard_map.97 = f32[2,1024]{1,0:T(2,128)} custom-call(bf16[2,512,512]{2,1,0:T(8,128)(2,1)} %get-tuple-element.8.parts, f32[512,512]{1,0:T(8,128)} %get-tuple-element.9.own, f32[8,8,1024]{2,1,0:T(8,128)} %get-tuple-element.10.spots, f32[2,1024]{1,0:T(2,128)} %momentum.1), custom_call_target="tpu_custom_call" | custom-call | tf_op jit(solution)/shard_map/pallas_call | solution.py:466
  84.7 0.0 slice-done
  84.7 0.0 copy-done
  84.7 0.0 copy-start.1
  84.7 1.5 %pad_maximum_fusion = bf16[8,256,512]{2,1,0:T(8,128)(2,1)} fusion(bf16[4,256,512]{2,1,0:T(8,128)(2,1)S(1)} %slice-done, bf16[4,256,512]{2,1,0:T(8,128)(2,1)S(1)} %copy-done), kind=kLoop, calls=%fused_computation.1 | loop fusion | flops 1048576 | bytes 4194304 | tf_op jit(solution)/shard_map/concatenate | solution.py:483
  86.2 0.0 copy-done.1
  86.2 0.6 copy.14
Async XLA Ops:
  46.7 38.0 %slice-start = ((bf16[8,256,512]{2,1,0:T(8,128)(2,1)}), bf16[4,256,512]{2,1,0:T(8,128)(2,1)S(1)}, s32[]{:S(2)}) async-start(bf16[8,256,512]{2,1,0:T(8,128)(2,1)} %old_ref.1), calls=%async_computation | async-start | bytes 2097152 | tf_op jit(solution)/shard_map/slice | solution.py:483
  46.7 38.0 %copy-start = (bf16[4,256,512]{2,1,0:T(8,128)(2,1)S(1)}, bf16[4,256,512]{2,1,0:T(8,128)(2,1)}, u32[]{:S(2)}) copy-start(bf16[4,256,512]{2,1,0:T(8,128)(2,1)} %get-tuple-element.11) | copy-start | bytes 3145732
  84.7 1.5 %copy-start.1 = (f32[2,1024]{1,0:T(2,128)S(1)}, f32[2,1024]{1,0:T(2,128)}, u32[]{:S(2)}) copy-start(f32[2,1024]{1,0:T(2,128)} %shard_map.97) | copy-start | bytes 24580
where the time goes:
time: 87.1 us; the launch traced here: 86.8 us
  Pallas kernels  77.7 us (89%)
  local copies, waits for them, and re-layouts  5.59 us (6%)
  other arithmetic  2.78 us (3%)
    pallas_call x1, Pallas kernels, sum_and_kick(): pl.pallas_call(functools.partial(sum_kernel, hist, rows, dom), out_shape=...  38 us
    pallas_call x1, Pallas kernels, field_parts(): pl.pallas_call(functools.partial(field_kernel, hist, rows, dom), out_shap...  25.6 us
    pallas_call x1, Pallas kernels, deposit(): pl.pallas_call(functools.partial(gather_kernel, rows, dom), out_shape=(ja...  14.1 us
    unnamed x6, local copies, waits for them, and re-layouts  5.58 us

commit v1 on v0

v1 whole, which is shorter than its diff:
```python
import functools
import jax
import jax.numpy as jnp
from jax import lax
from jax.experimental import pallas as pl
from jax.experimental.pallas import tpu as pltpu
from jax.sharding import PartitionSpec as P

NG = 512
BINS = 16
STEPS = 4
CORES = 2
HALVES = 4
kick_scale = 0.5

MESH = pl.DeviceIdType.MESH
VM = pl.BlockSpec(memory_space=pltpu.VMEM)
NT = (((1,), (1,)), ((), ()))


def place():
    return lax.axis_index("hist"), lax.axis_index("rows"), lax.axis_index("dom")


def hat(extent, whole, near, far):
    kind = jnp.bfloat16
    places = lax.broadcasted_iota(jnp.int32, (extent, whole.shape[1]), 0).astype(kind)
    first = whole.astype(kind)
    return jnp.where(places == first, near.astype(kind),
                     jnp.where(places == first + kind(1.0), far.astype(kind), kind(0.0)))


def plane_peer(rows, dom, shift):
    h, r, d = place()
    other = lax.rem(r * dom + d + shift, rows * dom)
    return other, (h, other // dom, lax.rem(other, dom))


def inside(index, count):
    return jnp.logical_and(index >= 0, index < count)


def kernel(hist, rows, dom, row_ref, col_ref, bin_ref, charge_ref, momentum, old_ref, cols_ref, rows_ref,
           out, newest, spots, base, frac, dens, summed, arrived, gath, grids, cols, raw, turned, total,
           parts, got, mine, from_low, from_high, to_high, to_low, kicks, got_kicks, load,
           sem_as, sem_ar, sem_hs, sem_hr, sem_cs, sem_cr, sem_xs, sem_xr, sem_ps, sem_pr, sem_fs, sem_fr,
           sem_ys, sem_yr, sem_us, sem_ur, sem_ds, sem_dr, sem_ks, sem_kr):
    h, r, d = place()
    n = rows * dom
    lags, width, _ = cols.shape
    band = old_ref.shape[1]
    piece = NG // rows
    size = width // HALVES
    kind = parts.dtype
    chips = dom // CORES
    up, down = (h + 1, r, d), (h - 1, r, d)
    levels = (hist - 1).bit_length()
    sums = [jnp.logical_and(lax.rem(h, 2 << a) == 0, h + (1 << a) < hist) for a in range(levels)]
    gives = [lax.rem(h, 2 << a) == 1 << a for a in range(levels)]
    rank = sum(jnp.where(lax.rem(h, 1 << a) == 0, 1, 0) for a in range(1, levels + 1))
    partner = (h, r, d + 1 - 2 * lax.rem(d, CORES))
    across = [(h, r, lax.rem(d + CORES * j, dom)) for j in range(1, chips)]
    is_first, is_last = h == 0, h == hist - 1
    below, above = jnp.logical_not(is_last), jnp.logical_not(is_first)
    inner = jnp.logical_and(below, above)

    loads = (pltpu.make_async_copy(old_ref, grids.at[pl.ds(STEPS, lags)], load.at[0]),
             pltpu.make_async_copy(cols_ref, cols, load.at[1]),
             pltpu.make_async_copy(rows_ref, raw, load.at[2]))
    for copy in loads:
        copy.start()
    barrier = pltpu.get_barrier_semaphore()

    @pl.when(below)
    def _():
        pl.semaphore_signal(barrier, inc=1, device_id=up, device_id_type=MESH)

    @pl.when(above)
    def _():
        pl.semaphore_signal(barrier, inc=1, device_id=down, device_id_type=MESH)

    for shift in range(1, n):
        pl.semaphore_signal(barrier, inc=1, device_id=plane_peer(rows, dom, shift)[1], device_id_type=MESH)
    count = n - 1 + jnp.where(is_first, 0, 1) + jnp.where(is_last, 0, 1)
    for a in range(1, levels):
        count += jnp.where(jnp.logical_or(sums[a], gives[a]), 1, 0)

        @pl.when(sums[a])
        def _():
            pl.semaphore_signal(barrier, inc=1, device_id=(h + (1 << a), r, d), device_id_type=MESH)

        @pl.when(gives[a])
        def _():
            pl.semaphore_signal(barrier, inc=1, device_id=(h - (1 << a), r, d), device_id_type=MESH)

    bins = bin_ref[...]
    row_bin = bins // BINS
    spots[0, 0:STEPS] = row_ref[...].astype(jnp.float32) + (row_bin.astype(jnp.float32) + 0.5) / BINS
    spots[0, STEPS:2 * STEPS] = (col_ref[...].astype(jnp.float32)
                                 + ((bins - row_bin * BINS).astype(jnp.float32) + 0.5) / BINS)
    spots[0, 2 * STEPS:] = charge_ref[...].astype(jnp.float32).reshape(1, -1)
    pl.semaphore_wait(barrier, count)

    def remote(src, dst, s_sem, r_sem, device):
        return pltpu.make_async_remote_copy(src_ref=src, dst_ref=dst, send_sem=s_sem, recv_sem=r_sem,
                                            device_id=device, device_id_type=MESH)

    def spot_copy(shift):
        return remote(spots.at[0], spots.at[shift], sem_as.at[shift], sem_ar.at[shift],
                      plane_peer(rows, dom, shift)[1])

    def tail_copy(s):
        columns = pl.ds(pl.multiple_of(d * width, width), width)
        return remote(old_ref.at[lags - 1 - s, :, columns], gath.at[d, s], sem_hs.at[s], sem_hr.at[s], up)

    def tree_copy(s, a):
        return remote(summed.at[s], arrived.at[s, a], sem_cs.at[s, a], sem_cr.at[s, a], (h - (1 << a), r, d))

    def cross_copy(s, j):
        return remote(gath.at[d, s], gath.at[d, s], sem_xs.at[s, j], sem_xr.at[s, j], across[j - 1])

    def partner_copy(s):
        return remote(gath.at[d, s], gath.at[d, s], sem_ps.at[s], sem_pr.at[s], partner)

    def forward_copy(s, j):
        other = lax.rem(d + CORES * (chips - j), dom)
        return remote(gath.at[other, s], gath.at[other, s], sem_fs.at[s, j], sem_fr.at[s, j], partner)

    def span(c):
        return pl.ds(pl.multiple_of(c * size, size), size)

    def row_copy(c, j):
        other = lax.rem(r + j, rows)
        return remote(parts.at[other, span(c)], got.at[j, span(c)], sem_ys.at[c, j], sem_yr.at[c, j],
                      (h, other, d))

    def up_copy(c):
        return remote(to_high.at[span(c)], from_low.at[span(c)], sem_us.at[c], sem_ur.at[c], up)

    def down_copy(c):
        return remote(to_low.at[span(c)], from_high.at[span(c)], sem_ds.at[c], sem_dr.at[c], down)

    def kick_copy(k):
        return remote(kicks.at[k], got_kicks.at[k], sem_ks.at[k], sem_kr.at[k], plane_peer(rows, dom, n - k)[1])

    for shift in range(1, n):
        spot_copy(shift).start()

    @pl.when(below)
    def _():
        for s in range(STEPS):
            tail_copy(s).start()

    total[...] = jnp.zeros_like(total)
    dens[...] = jnp.zeros_like(dens)
    kicks[...] = jnp.zeros_like(kicks)
    for copy in loads:
        copy.wait()

    def add_field(weights, mixed, where):
        for comp in range(2):
            total[comp, where] += jnp.dot(mixed, weights[comp], preferred_element_type=jnp.float32)

    def products(k, weights, start, steps):
        window = grids[pl.ds(start, steps)].reshape(steps * band, NG)
        mixed = lax.dot_general(cols[k], window, NT, preferred_element_type=jnp.float32).astype(kind)
        stacked = jnp.concatenate(
            [mixed[:, (steps - 1 - s) * band:(steps - s) * band] for s in range(steps)], axis=0)
        add_field(weights, stacked, pl.ds(0, steps * width))

    def whole_lag(k):
        products(k, pltpu.einshape("acb->cab", raw[k]), k, STEPS)

    ahead = max(0, lags - STEPS - 2)

    def lag(k, carry):
        whole_lag(k)
        return carry

    lax.fori_loop(STEPS, STEPS + ahead, lag, 0)
    turned[0] = pltpu.einshape("acb->cab", raw[0])
    for k in range(1, STEPS):
        turned[k] = pltpu.einshape("acb->cab", raw[k])
        products(k, turned[k], STEPS, k)

    side = lax.broadcasted_iota(jnp.int32, (2 * STEPS, 1), 0)
    corner = jnp.where(side < STEPS, r * band, d * width).astype(jnp.float32)

    def settle(k):
        value = spots[k, 0:2 * STEPS]
        floor = jnp.floor(value)
        base[k] = floor - corner
        frac[k] = value - floor

    settle(0)

    def arrive(k, carry):
        spot_copy(k).wait_recv()
        settle(k)
        return carry

    lax.fori_loop(1, n, arrive, 0)

    def row_of(k, s):
        return base[k, pl.ds(s, 1), :], frac[k, pl.ds(s, 1), :]

    def deposit(s):
        def block(k, carry):
            charge = spots[k, 2 * STEPS:, :]
            row, up_row = row_of(k, s)
            col, up_col = row_of(k, STEPS + s)
            left = hat(band, row, charge * (1.0 - up_row), charge * up_row)
            right = hat(width, col, 1.0 - up_col, up_col)
            dens[s] += lax.dot_general(left, right, NT, preferred_element_type=jnp.float32)
            return carry

        lax.fori_loop(0, n, block, 0, unroll=4)

    def relay(s):
        for a in range(levels):
            @pl.when(sums[a])
            def _():
                tree_copy(s, a).wait_recv()
                dens[s] += arrived[s, a].astype(jnp.float32)

        @pl.when(is_first)
        def _():
            gath[d, s] = dens[s].astype(kind)

        @pl.when(above)
        def _():
            summed[s] = dens[s].astype(kind)

        for a in range(levels):
            @pl.when(gives[a])
            def _():
                tree_copy(s, a).start()

    def gather(s):
        @pl.when(above)
        def _():
            tail_copy(s).wait_recv()

        for j in range(1, chips):
            cross_copy(s, j).start()
        partner_copy(s).start()

    def forward(s):
        for j in range(1, chips):
            cross_copy(s, j).wait_recv()
            forward_copy(s, j).start()

    def late(s):
        partner_copy(s).wait_recv()
        for j in range(1, chips):
            forward_copy(s, j).wait_recv()
        grid = jnp.concatenate([gath[e, s] for e in range(dom)], axis=1)
        grids[STEPS - 1 - s] = grid
        newest[STEPS - 1 - s] = grid
        where = pl.ds(pl.multiple_of(s * width, width), width)

        def add(k, carry):
            mixed = lax.dot_general(cols[k], grids[STEPS - 1 - s + k], NT,
                                    preferred_element_type=jnp.float32).astype(kind)
            add_field(turned[k], mixed, where)
            return carry

        lax.fori_loop(0, s + 1, add, 0)
        for q in range(rows):
            block = jnp.concatenate([total[comp, where, q * piece:(q + 1) * piece] for comp in range(2)], axis=1)

            @pl.when(r == q)
            def _():
                mine[where] = block

            @pl.when(r != q)
            def _():
                parts[q, where] = block.astype(kind)

        for half in range(HALVES):
            for j in range(1, rows):
                row_copy(s * HALVES + half, j).start()

    def spread(s):
        for half in range(HALVES):
            c = s * HALVES + half
            value = mine[span(c)]
            for j in range(1, rows):
                row_copy(c, j).wait_recv()
                value += got[j, span(c)].astype(jnp.float32)
            mine[span(c)] = value

            @pl.when(is_first)
            def _():
                to_high[span(c)] = value.astype(kind)
                up_copy(c).start()

            @pl.when(is_last)
            def _():
                to_low[span(c)] = value.astype(kind)
                down_copy(c).start()

    def rise(s):
        for half in range(HALVES):
            c = s * HALVES + half
            up_copy(c).wait_recv()

            @pl.when(inner)
            def _():
                to_high[span(c)] = (mine[span(c)] + from_low[span(c)].astype(jnp.float32)).astype(kind)
                up_copy(c).start()

    def sink(s):
        for half in range(HALVES):
            c = s * HALVES + half
            down_copy(c).wait_recv()

            @pl.when(inner)
            def _():
                to_low[span(c)] = (mine[span(c)] + from_high[span(c)].astype(jnp.float32)).astype(kind)
                down_copy(c).start()

    def kick(s):
        where = pl.ds(pl.multiple_of(s * width, width), width)

        @pl.when(above)
        def _():
            mine[where] = mine[where] + from_low[where].astype(jnp.float32)

        @pl.when(below)
        def _():
            mine[where] = mine[where] + from_high[where].astype(jnp.float32)

        value = mine[where]
        table = jnp.concatenate([value[:, :band], value[:, band:]], axis=0).astype(kind)

        def block(k, carry):
            row, up_row = row_of(k, s)
            col, up_col = row_of(k, STEPS + s)
            left = hat(band, row, 1.0 - up_row, up_row)
            right = hat(width, col, 1.0 - up_col, up_col).astype(jnp.float32)
            along = jnp.dot(table, left, preferred_element_type=jnp.float32)
            for comp in range(2):
                kicks[k, comp:comp + 1, :] += jnp.sum(
                    along[comp * width:(comp + 1) * width] * right, axis=0, keepdims=True)
            return carry

        lax.fori_loop(0, n, block, 0, unroll=2)

    early, level = STEPS + 1, 2 * levels
    row_off = jnp.where(is_first, level + 4, early + 4)
    rise_off, sink_off = early + 6 + h, early + 5 + (hist - 1 - h)
    kick_off = jnp.maximum(rise_off, sink_off) + jnp.where(is_first, 0, 2 * (hist - 1 - h))

    def at(index, action):
        @pl.when(inside(index, STEPS))
        def _():
            action(index)

    def tick(t, carry):
        at(t, deposit)
        at(t - 2 * rank, relay)
        ready = jnp.where(is_first, t - level, t)
        at(ready, gather)
        at(t - row_off, spread)

        @pl.when(above)
        def _():
            at(t - rise_off, rise)

        @pl.when(below)
        def _():
            at(t - sink_off, sink)

        at(jnp.where(is_first, t - level - 2, t - early), late)
        at(ready - 1, forward)
        spare = t - (STEPS - 1) + STEPS + ahead

        @pl.when(jnp.logical_and(t >= STEPS - 1, spare < lags))
        def _():
            whole_lag(spare)

        at(t - kick_off, kick)
        return carry

    lax.fori_loop(0, STEPS + max(early + 5 + hist - 1, early + 6 + hist - 1, early + 5 + 3 * (hist - 2)
                                 + 1, early + 5 + hist), tick, 0)

    for k in range(1, n):
        kick_copy(k).start()
    for shift in range(1, n):
        spot_copy(shift).wait_send()
    for s in range(STEPS):
        partner_copy(s).wait_send()
        for j in range(1, chips):
            forward_copy(s, j).wait_send()
            cross_copy(s, j).wait_send()

    @pl.when(above)
    def _():
        for c in range(STEPS * HALVES):
            down_copy(c).wait_send()

    for a in range(levels):
        @pl.when(gives[a])
        def _():
            for s in range(STEPS):
                tree_copy(s, a).wait_send()

    @pl.when(below)
    def _():
        for s in range(STEPS):
            tail_copy(s).wait_send()
        for c in range(STEPS * HALVES):
            up_copy(c).wait_send()

    for c in range(STEPS * HALVES):
        for j in range(1, rows):
            row_copy(c, j).wait_send()
    sum_all = kicks[0]
    for k in range(1, n):
        kick_copy(k).wait()
        sum_all = sum_all + got_kicks[k]
    out[...] = momentum[...] + kick_scale * sum_all


def local(hist, rows, dom, row_index, col_index, bin_index, charge, momentum, history, kernel_cols, kernel_rows):
    lags, band, _ = history.shape
    width = kernel_cols.shape[1]
    own = row_index.shape[1]
    n = rows * dom
    chips, levels = dom // CORES, (hist - 1).bit_length()
    tall, wide = STEPS * width, 2 * NG // rows
    count = STEPS * HALVES
    kind, wider = jnp.bfloat16, jnp.float32
    dma, vmem = pltpu.SemaphoreType.DMA, pltpu.VMEM
    anywhere = pl.BlockSpec(memory_space=pl.ANY)
    tile = (STEPS, band, width)
    flat = vmem((tall, wide), kind)
    each = vmem((n,) + momentum.shape, wider)
    moved, newest = pl.pallas_call(
        functools.partial(kernel, hist, rows, dom),
        out_shape=(jax.ShapeDtypeStruct(momentum.shape, wider),
                   jax.ShapeDtypeStruct((STEPS, band, NG), kind)),
        in_specs=[VM] * 5 + [anywhere] * 3, out_specs=(VM, VM),
        scratch_shapes=[vmem((n, 2 * STEPS + 1, own), wider), vmem((n, 2 * STEPS, own), wider),
                        vmem((n, 2 * STEPS, own), wider), vmem(tile, wider), vmem(tile, kind), vmem((STEPS, levels) + tile[1:], kind),
                        vmem((dom,) + tile, kind), vmem((lags + STEPS, band, NG), kind),
                        vmem(kernel_cols.shape, kind), vmem(kernel_rows.shape, kind),
                        vmem((STEPS, 2, band, NG), kind), vmem((2, tall, NG), wider),
                        vmem((rows, tall, wide), kind), vmem((rows, tall, wide), kind), vmem((tall, wide), wider),
                        flat, flat, flat, flat, each, each, dma((3,)), dma((n,)), dma((n,))]
        + [dma((STEPS,))] * 2 + [dma((STEPS, levels))] * 2 + [dma((STEPS, chips))] * 2 + [dma((STEPS,))] * 2 + [dma((STEPS, chips))] * 2
        + [dma((count, rows))] * 2 + [dma((count,))] * 4 + [dma((n,))] * 2,
        compiler_params=pltpu.CompilerParams(collective_id=1, has_side_effects=True),
    )(row_index, col_index, bin_index, charge, momentum, history, kernel_cols, kernel_rows)
    return moved, jnp.concatenate([newest, history[:-STEPS]], axis=0)


def solution(mesh):
    spread = ("hist", "rows", "dom")
    in_specs = (P(None, spread), P(None, spread), P(None, spread), P(spread), P(None, spread),
                P("hist", "rows", None), P("hist", "dom", None), P("hist", "rows", None, None))
    out_specs = (P(None, spread), P("hist", "rows", None))
    sizes = mesh.shape
    body = functools.partial(local, sizes["hist"], sizes["rows"], sizes["dom"])
    return jax.shard_map(body, mesh=mesh, in_specs=in_specs, out_specs=out_specs, check_vma=False)
```

time: 87.1 us -> 69.5 us (0.80)
  the two profiles are of different devices: /device:TPU:0 before, /device:TPU:9 now
where the time goes in v1:
time: 69.5 us; the launch traced here: 69.3 us
  Pallas kernels  65.3 us (94%)
  other arithmetic  2.73 us (4%)
    pallas_call x1, Pallas kernels, local(): pl.pallas_call(functools.partial(kernel, hist, rows, dom), out_shape=(jax...  65.3 us
    concatenate x1, other arithmetic, local(): return (moved, jnp.concatenate([newest, history[:-STEPS]], axis=0))  2.73 us

profile of v1, /device:TPU:9, one launch (start us, length us, event | category | flops | bytes accessed | tf_op | source)
XLA Modules:
  0.0 69.3 jit_solution(14437759463309443400)
XLA Ops:
  0.6 0.0 slice-start
  0.6 65.3 %shard_map.95 = (f32[2,1024]{1,0:T(2,128)}, bf16[4,256,512]{2,1,0:T(8,128)(2,1)}) custom-call(s32[4,1024]{1,0:T(4,128)} %row_ref.1, s32[4,1024]{1,0:T(4,128)} %col_ref.1, s32[4,1024]{1,0:T(4,128)} %bin_ref.1, bf16[1024]{0:T(1024)(128)(2,1)} %charge_ref.1, f32[2,1024]{1,0:T(2,128)} %momentum.1, bf16[8,256,512]{2,1,0:T(8,128)(2,1)} %old_ref.1, ...), custom_call_target="tpu_custom_call" | custom-call | tf_op jit(solution)/shard_map/pallas_call | solution.py:441
  66.0 0.0 slice-done
  66.0 0.0 copy-start
  66.0 2.7 %pad_maximum_fusion = bf16[8,256,512]{2,1,0:T(8,128)(2,1)} fusion(bf16[4,256,512]{2,1,0:T(8,128)(2,1)S(1)} %slice-done, bf16[4,256,512]{2,1,0:T(8,128)(2,1)} %get-tuple-element.5), kind=kLoop, calls=%fused_computation | loop fusion | flops 1048576 | bytes 4194304 | tf_op jit(solution)/shard_map/concatenate | solution.py:457
  68.7 0.0 copy-done
  68.7 0.6 copy.11
Async XLA Ops:
  0.6 65.3 %slice-start = ((bf16[8,256,512]{2,1,0:T(8,128)(2,1)}), bf16[4,256,512]{2,1,0:T(8,128)(2,1)S(1)}, s32[]{:S(2)}) async-start(bf16[8,256,512]{2,1,0:T(8,128)(2,1)} %old_ref.1), calls=%async_computation | async-start | bytes 2097152 | tf_op jit(solution)/shard_map/slice | solution.py:457
  66.0 2.7 %copy-start = (f32[2,1024]{1,0:T(2,128)S(1)}, f32[2,1024]{1,0:T(2,128)}, u32[]{:S(2)}) copy-start(f32[2,1024]{1,0:T(2,128)} %get-tuple-element.8) | copy-start | bytes 24580
